TPU v7x, 32 devices: a whole 2x2x4 slice. The times are simulated.
32 devices in a mesh: kv: 2 (over x), dup: 16 (over z, y, core).
Axes of the slice: x: 2, y: 2, z: 4, core: 2. Of those that a mesh axis runs over, the one named last changes fastest.
Arguments:
- queries: bfloat16 [512, 48, 128], P('kv', 'dup'), parts along dimension 0
- key_cache: bfloat16 [512, 4096, 128], P('kv', 'dup'), parts along dimension 0
- value_cache: bfloat16 [512, 4096, 128], P('kv', 'dup'), parts along dimension 0
- lengths: int32 [512], P('kv'), parts along dimension 0
Outputs:
- output: bfloat16 [512, 48, 128], P('kv', 'dup'), parts along dimension 0
There are 2 independent parts. A program takes and returns all parts, laid end to end along the dimension named above; each array names one.
All inputs are finite; a program needn't handle non-finite values.
Results may differ from a plain program's by a relative error of at most 0.00813525.
Values are sent between devices in bfloat16 or wider.
A program may use at most 1 GiB of HBM per device.

v0:
```python
import jax
import jax.numpy as jnp
from jax import lax
from jax.sharding import PartitionSpec as P, NamedSharding

DRAFT = 4
NEG_BIG = -1e30


def solution(mesh):
    dup_size = mesh.shape["dup"]

    def group_step(q_local, k_span, v_span, len_local):
        num_batch, span_len, head_dim = k_span.shape
        span_start = lax.axis_index("dup") * span_len
        q_group = lax.all_gather(q_local, "dup", axis=1, tiled=True)
        num_rows = q_group.shape[1]
        own_rows = num_rows // dup_size
        scores = jnp.einsum("brd,bsd->brs", q_group, k_span, preferred_element_type=jnp.float32) * (head_dim ** -0.5)
        last_pos = len_local[:, None] - DRAFT + (jnp.arange(num_rows) % DRAFT)[None, :]
        allowed = (span_start + jnp.arange(span_len))[None, None, :] <= last_pos[:, :, None]
        scores = jnp.where(allowed, scores, NEG_BIG)
        row_peak = jnp.max(scores, axis=2, keepdims=True)
        prob_vals = jnp.exp(scores - row_peak)
        row_mass = jnp.sum(prob_vals, axis=2, keepdims=True)
        weighted = jnp.einsum("brs,bsd->brd", prob_vals.astype(jnp.bfloat16), v_span, preferred_element_type=jnp.float32)
        part_out = (weighted / row_mass).astype(jnp.bfloat16).reshape(num_batch, dup_size, own_rows, head_dim)
        log_mass = (row_peak + jnp.log(row_mass)).reshape(num_batch, dup_size, own_rows)
        recv_out = lax.all_to_all(part_out, "dup", 1, 1)
        recv_mass = lax.all_to_all(log_mass, "dup", 1, 1)
        top_mass = jnp.max(recv_mass, axis=1, keepdims=True)
        weights = jnp.exp(recv_mass - top_mass)
        total_mass = jnp.sum(weights, axis=1)
        merged = jnp.sum(weights[..., None] * recv_out.astype(jnp.float32), axis=1)
        return (merged / total_mass[..., None]).astype(jnp.bfloat16)

    return jax.shard_map(group_step, mesh=mesh, in_specs=(P("kv", "dup", None), P("kv", "dup", None), P("kv", "dup", None), P("kv")), out_specs=P("kv", "dup", None), check_vma=False)
```

profile of v0, /device:TPU:13, one launch (start us, length us, event | category | flops | bytes accessed | tf_op | source)
XLA Modules:
  0.0 181.9 jit_solution(14031233903553184300)
XLA Ops:
  6.5 0.0 all-gather.2.cloned.1.call-start
  6.5 0.7 all-gather.2.cloned.1.call-update
  7.3 0.7 broadcast_add_fusion.1
  8.0 0.1 broadcast_add_fusion
  8.1 47.3 %all-gather.2.cloned.1.call-done = bf16[256,48,128]{2,0,1:T(8,128)(2,1)} async-done(((bf16[256,3,128]{2,0,1:T(8,128)(2,1)}), bf16[256,48,128]{2,0,1:T(8,128)(2,1)}) %all-gather.2.cloned.1.call-update) | async-done | bytes 3145744 | tf_op jit(solution)/shard_map/all_gather | solution.py:16
  55.4 12.9 %fusion.2 = (f32[256,48]{1,0:T(8,128)S(1)}, f32[256,48,256]{2,1,0:T(8,128)}) fusion(s32[256,48]{1,0:T(8,128)S(1)} %broadcast_add_fusion, s32[256]{0:T(256)S(1)} %iota_add_fusion, bf16[256,256,128]{2,1,0:T(8,128)(2,1)} %param.5, bf16[256,48,128]{2,0,1:T(8,128)(2,1)} %all-gather.2.cloned.1.call-done), kind=kOutput, calls=%fused_computation.4 | convolution fusion | flops 817876992 | bytes 32605184 | tf_op jit(solution)/shard_map/brd,bsd->brs/dot_general | solution.py:19
  68.3 7.4 %fusion.1 = f32[256,48]{1,0:T(8,128)S(1)} fusion(f32[256,48,256]{2,1,0:T(8,128)} %get-tuple-element.8, f32[256,48]{1,0:T(8,128)S(1)} %get-tuple-element.7, s32[256,48]{1,0:T(8,128)S(1)} %broadcast_add_fusion, s32[256]{0:T(256)S(1)} %iota_add_fusion), kind=kLoop, calls=%fused_computation.3 | loop fusion | flops 15716352 | bytes 12731392 | tf_op jit(solution)/shard_map/reduce_sum | solution.py:25
  75.7 0.1 copy.11
  75.8 0.7 add.55
  76.5 4.9 %all-to-all-start = ((f32[256,16,3]{0,2,1:T(4,128)}), f32[256,16,3]{0,2,1:T(4,128)S(1)}, u32[]{:S(2)}, u32[]{:S(2)}) async-start(f32[256,16,3]{0,2,1:T(4,128)} %add.55), calls=%async_computation | async-start | bytes 131072 | tf_op jit(solution)/shard_map/all_to_all | solution.py:30
  81.4 12.1 %divide_convert_fusion = bf16[256,48,128]{2,1,0:T(8,128)(2,1)S(1)} fusion(f32[256,48]{1,0:T(8,128)S(1)} %fusion.1, bf16[256,256,128]{2,1,0:T(8,128)(2,1)} %param.6, f32[256,48,256]{2,1,0:T(8,128)} %get-tuple-element.8, f32[256,48]{1,0:T(8,128)S(1)} %get-tuple-element.7, s32[256,48]{1,0:T(8,128)S(1)} %broadcast_add_fusion, s32[256]{0:T(256)S(1)} %iota_add_fusion), kind=kOutput, calls=%fused_computation.7 | convolution fusion | flops 824180736 | bytes 32654336 | tf_op jit(solution)/shard_map/brs,bsd->brd/dot_general | solution.py:26
  93.5 2.5 %copy.12 = bf16[256,48,128]{2,0,1:T(8,128)(2,1)} copy(bf16[256,48,128]{2,1,0:T(8,128)(2,1)S(1)} %divide_convert_fusion) | data formatting | bytes 6291456 | tf_op jit(solution)/shard_map/convert_element_type | solution.py:27
  96.0 0.0 all-to-all-done
  96.0 6.1 %all-to-all-start.1 = ((bf16[256,16,3,128]{3,0,2,1:T(8,128)(2,1)}), bf16[256,16,3,128]{3,0,2,1:T(8,128)(2,1)S(1)}, u32[]{:S(2)}, u32[]{:S(2)}) async-start(bf16[256,16,3,128]{3,0,2,1:T(8,128)(2,1)} %bitcast), calls=%async_computation.1 | async-start | bytes 6291456 | tf_op jit(solution)/shard_map/all_to_all | solution.py:29
  102.1 70.1 %all-to-all-done.1 = bf16[256,16,3,128]{3,0,2,1:T(8,128)(2,1)S(1)} async-done(((bf16[256,16,3,128]{3,0,2,1:T(8,128)(2,1)}), bf16[256,16,3,128]{3,0,2,1:T(8,128)(2,1)S(1)}, u32[]{:S(2)}, u32[]{:S(2)}) %all-to-all-start.1) | async-done | bytes 3145760 | tf_op jit(solution)/shard_map/all_to_all | solution.py:29
  172.2 1.9 %multiply_reduce_fusion = f32[256,3,128]{2,0,1:T(8,128)S(1)} fusion(bf16[256,16,3,128]{3,0,2,1:T(8,128)(2,1)S(1)} %all-to-all-done.1, f32[256,16,3]{0,2,1:T(4,128)S(1)} %get-tuple-element.6), kind=kLoop, calls=%fused_computation.6 | loop fusion | flops 4620288 | bytes 3588096 | tf_op jit(solution)/shard_map/reduce_sum | solution.py:34
  174.2 0.9 divide_convert_fusion.1
  (5 shorter events, 0.1 us)
Async XLA Ops:
  6.5 48.8 %all-gather.2.cloned.1.call-start = ((), (), s32[]{:S(2)}) async-start(), calls=%async_computation.2 | async-start | bytes 3342336 | tf_op jit(solution)/shard_map/all_gather | solution.py:16
  76.5 19.5 %all-to-all-start = ((f32[256,16,3]{0,2,1:T(4,128)}), f32[256,16,3]{0,2,1:T(4,128)S(1)}, u32[]{:S(2)}, u32[]{:S(2)}) async-start(f32[256,16,3]{0,2,1:T(4,128)} %add.55), calls=%async_computation | async-start | bytes 131072 | tf_op jit(solution)/shard_map/all_to_all | solution.py:30
  96.0 76.2 %all-to-all-start.1 = ((bf16[256,16,3,128]{3,0,2,1:T(8,128)(2,1)}), bf16[256,16,3,128]{3,0,2,1:T(8,128)(2,1)S(1)}, u32[]{:S(2)}, u32[]{:S(2)}) async-start(bf16[256,16,3,128]{3,0,2,1:T(8,128)(2,1)} %bitcast), calls=%async_computation.1 | async-start | bytes 6291456 | tf_op jit(solution)/shard_map/all_to_all | solution.py:29
Sparse Core Ops, SparseCore 0:
  9.6 45.7 all-gather.1
where the time goes:
time: 182 us
  waiting for transfers between devices  118 us (65%)
  matrix products  25.1 us (14%)
  between operations  13.5 us (7%)
  other arithmetic  11.1 us (6%)
  starting transfers between devices  11 us (6%)
  local copies, waits for them, and re-layouts  3.21 us (2%)
    all_to_all x1, waiting for transfers between devices, group_step(): recv_out = lax.all_to_all(part_out, 'dup', 1, 1)  70.1 us
    all_gather x1, waiting for transfers between devices, group_step(): q_group = lax.all_gather(q_local, 'dup', axis=1, tiled=True)  47.3 us
    dot_general x1, matrix products, group_step(): jnp.einsum('brd,bsd->brs', q_group, k_span, preferred_element_type=jnp.fl...  12.9 us
    dot_general x1, matrix products, group_step(): jnp.einsum('brs,bsd->brd', prob_vals.astype(jnp.bfloat16), v_span, prefer...  12.1 us
    reduce_sum x1, other arithmetic, group_step(): row_mass = jnp.sum(prob_vals, axis=2, keepdims=True)  7.37 us
    all_to_all x1, starting transfers between devices, group_step(): recv_out = lax.all_to_all(part_out, 'dup', 1, 1)  6.06 us
    all_to_all x1, starting transfers between devices, group_step(): recv_mass = lax.all_to_all(log_mass, 'dup', 1, 1)  4.9 us
  transfers between devices with their start and end apart: 3, of which 2 were waited for; matrix products, arithmetic and copies ran while one was open for 9% of the time, Pallas kernels for 0%

commit v1 on v0

v1 whole, which is shorter than its diff:
```python
import functools
import math

import jax
import jax.numpy as jnp
from jax import lax
from jax.experimental import pallas as pl
from jax.experimental.pallas import tpu as pltpu
from jax.sharding import PartitionSpec as P

DRAFT = 4
CHUNKS = 8
UNROLL = 4
NEG = -3.4e38
FLOOR = -3.0e38
MESH = pl.DeviceIdType.MESH
F32 = jnp.float32
BF16 = jnp.bfloat16


def fused(nb, own, span, dim, len_ref, q_ref, k_ref, v_ref, out_ref,
          kbuf, vbuf, qbuf, qf, of, posm, macc, laccs,
          p1s, p1r, e1s, e1k, e1r, p2s, p2k, p2r, e2s, e2k, e2r, p3s, p3k, p3r, e3s, e3k, e3r,
          wtmp, kvsem, qsem, gs, gr, rs, rr):
    nc = CHUNKS
    bc = nb // nc
    pitch = bc + 8
    rows = 16 * own
    half, quar = rows // 2, rows // 4
    scale = dim ** -0.5
    me = lax.axis_index("dup")
    core, yy, zz = me % 2, (me // 2) % 2, me // 4
    partner = me + 1 - 2 * core
    ypeer = me + 2 - 4 * yy
    zpeer = [None,
             me + 4 * (1 - 2 * (zz % 2)),
             me + 4 * (2 - 4 * (zz // 2)),
             me + 4 * (3 - 2 * zz)]

    def kv_copies(c):
        sl = pl.ds(c * bc, bc)
        return (pltpu.make_async_copy(k_ref.at[sl], kbuf.at[sl], kvsem.at[0, c]),
                pltpu.make_async_copy(v_ref.at[sl], vbuf.at[sl], kvsem.at[1, c]))

    def own_q(c):
        return pltpu.make_async_copy(q_ref.at[:, pl.ds(c * bc, bc)], qbuf.at[c, 0], qsem.at[c])

    def remote(src, dst, ssem, rsem, dev):
        return pltpu.make_async_remote_copy(src_ref=src, dst_ref=dst, send_sem=ssem, recv_sem=rsem,
                                            device_id={"dup": dev}, device_id_type=MESH)

    def send_own(c, slot, dev, idx):
        return remote(q_ref.at[:, pl.ds(c * bc, bc)], qbuf.at[c, slot], gs.at[idx, c], gr.at[slot, c], dev)

    def forward(c, slot_from, slot_to, dev, idx):
        return remote(qbuf.at[c, slot_from], qbuf.at[c, slot_to], gs.at[idx, c], gr.at[slot_to, c], dev)

    def own_sends(c):
        return ([send_own(c, k, zpeer[k], k) for k in (1, 2, 3)]
                + [send_own(c, 4, ypeer, 4), send_own(c, 8, partner, 8)])

    def z_forwards(c, k):
        return [forward(c, k, 4 + k, ypeer, 4 + k), forward(c, k, 8 + k, partner, 8 + k)]

    def y_forwards(c, k):
        return [forward(c, 4 + k, 12 + k, partner, 12 + k)]

    def wait_slot(c, slot):
        forward(c, slot, slot, partner, 0).wait_recv()

    def r1_copies(c):
        return [remote(p1s.at[c], p1r.at[c], rs.at[0, c], rr.at[0, c], partner),
                remote(e1s.at[c], e1r.at[c], rs.at[1, c], rr.at[1, c], partner)]

    def r2_copies(c):
        return [remote(p2s.at[c], p2r.at[c], rs.at[2, c], rr.at[2, c], ypeer),
                remote(e2s.at[c], e2r.at[c], rs.at[3, c], rr.at[3, c], ypeer)]

    def r3_copies(c):
        out = []
        for k in (1, 2, 3):
            out.append(remote(p3s.at[c, k - 1], p3r.at[c, k - 1], rs.at[2 + 2 * k, c], rr.at[2 + 2 * k, c], zpeer[k]))
            out.append(remote(e3s.at[c, k - 1], e3r.at[c, k - 1], rs.at[3 + 2 * k, c], rr.at[3 + 2 * k, c], zpeer[k]))
        return out

    def prefetch(c, carry):
        own_q(c).start()
        for cp in kv_copies(c):
            cp.start()
        return carry

    lax.fori_loop(0, nc, prefetch, 0)

    barrier = pltpu.get_barrier_semaphore()
    peers = (partner, ypeer, zpeer[1], zpeer[2], zpeer[3])
    for dev in peers:
        pl.semaphore_signal(barrier, inc=1, device_id={"dup": dev}, device_id_type=MESH)
    pl.semaphore_wait(barrier, len(peers))

    rowid = lax.broadcasted_iota(jnp.int32, (rows, span), 0)
    lane = lax.broadcasted_iota(jnp.int32, (rows, span), 1)
    slot = (rowid * 171) >> 9
    item = rowid - 3 * slot
    rel = (slot & 3) * 4 + ((slot >> 2) & 1) * 2 + (slot >> 3)
    tok = (own * (rel ^ me) + item) & 3
    posm[...] = me * span + lane + 4 - tok
    for ref in (e1s, e2s, e3s, e3k, e1k, e2k):
        ref[...] = jnp.zeros_like(ref)
    wtmp[...] = jnp.zeros_like(wtmp)

    def g1(c):
        for cp in own_sends(c):
            cp.start()

    def g2(c):
        for k in (1, 2, 3):
            wait_slot(c, k)
            for cp in z_forwards(c, k):
                cp.start()

    def g3(c):
        for k in range(4):
            wait_slot(c, 4 + k)
            for cp in y_forwards(c, k):
                cp.start()

    def compute(c):
        for s in range(8, 16):
            wait_slot(c, s)
        own_q(c).wait()
        for s in range(16):
            for i in range(own):
                qf[pl.ds((s * own + i) * pitch, bc), :] = qbuf[c, s, i].astype(F32)
        for cp in kv_copies(c):
            cp.wait()
        base = (c % 2) * (rows * pitch)
        macc[...] = jnp.zeros_like(macc)
        laccs[...] = jnp.ones_like(laccs)
        lanes = lax.broadcasted_iota(jnp.int32, (rows, 128), 1)

        def group(g, carry):
            mv, lv = macc[...], laccs[...]
            for u in range(UNROLL):
                j = g * UNROLL + u
                b = c * bc + j
                qb = qf[pl.ds(j, rows, stride=pitch), :].astype(BF16)
                s = lax.dot_general(qb, kbuf[b], (((1,), (1,)), ((), ())), preferred_element_type=F32)
                s = jnp.where(posm[...] <= len_ref[b], s, NEG)
                mx = jnp.maximum(jnp.max(s, axis=1, keepdims=True), FLOOR)
                p = jnp.exp2((s - mx) * (scale * math.log2(math.e)))
                den = jnp.maximum(jnp.sum(p, axis=1, keepdims=True), 1.0)
                o = jnp.dot(p.astype(BF16), vbuf[b], preferred_element_type=F32) * (1.0 / den)
                of[pl.ds(base + j, rows, stride=pitch), :] = o
                hit = lanes == j
                mv = jnp.where(hit, mx, mv)
                lv = jnp.where(hit, den, lv)
            macc[...] = mv
            laccs[...] = lv
            return carry

        lax.fori_loop(0, bc // UNROLL, group, 0)
        lse = macc[...] * scale + jnp.log(laccs[...])
        e1s[c] = lse[half:]
        e1k[c] = lse[:half]
        for r in range(half):
            p1s[c, r] = of[pl.ds(base + (half + r) * pitch, bc), :].astype(BF16)
        for cp in r1_copies(c):
            cp.start()

    def merge(a, b):
        top = jnp.maximum(a, b)
        ea, eb = jnp.exp(a - top), jnp.exp(b - top)
        tot = ea + eb
        return eb / tot, top + jnp.log(tot)

    def r2(c):
        for cp in r1_copies(c):
            cp.wait_recv()
        base = (c % 2) * (rows * pitch)
        w, lse = merge(e1k[c], e1r[c])
        e2k[c] = lse[:quar]
        e2s[c] = lse[quar:]
        wt = w.T
        for r in list(range(quar, half)) + list(range(quar)):
            wb = wt[:bc, r:r + 1]
            o1 = of[pl.ds(base + r * pitch, bc), :]
            o = (1.0 - wb) * o1 + wb * p1r[c, r].astype(F32)
            if r < quar:
                p2k[c, r] = o
            else:
                p2s[c, r - quar] = o.astype(BF16)
        for cp in r2_copies(c):
            cp.start()

    def r3(c):
        for cp in r2_copies(c):
            cp.wait_recv()
        w, lse = merge(e2k[c], e2r[c])
        for k in range(4):
            if k:
                e3s[c, k - 1, 0:own] = lse[k * own:(k + 1) * own]
            else:
                e3k[c, 0:own] = lse[:own]
        wtmp[0:quar] = w
        wt = wtmp[...].T
        for r in list(range(own, quar)) + list(range(own)):
            wb = wt[:bc, r:r + 1]
            o = (1.0 - wb) * p2k[c, r] + wb * p2r[c, r].astype(F32)
            if r < own:
                p3k[c, r] = o
            else:
                p3s[c, r // own - 1, r % own] = o.astype(BF16)
        for cp in r3_copies(c):
            cp.start()

    def r4(c):
        for cp in r3_copies(c):
            cp.wait_recv()
        ls = [e3k[c]] + [e3r[c, k] for k in range(3)]
        top = jnp.maximum(jnp.maximum(ls[0], ls[1]), jnp.maximum(ls[2], ls[3]))
        es = [jnp.exp(x - top) for x in ls]
        inv = 1.0 / (es[0] + es[1] + es[2] + es[3])
        for k in range(4):
            wtmp[4 * k:4 * k + 4] = es[k] * inv
        wt = wtmp[...].T
        for i in range(own):
            o = wt[:bc, i:i + 1] * p3k[c, i]
            for k in range(3):
                o = o + wt[:bc, 4 * k + 4 + i:4 * k + 5 + i] * p3r[c, k, i].astype(F32)
            out_ref[i, pl.ds(c * bc, bc)] = o.astype(BF16)

    g1(0)
    g1(1)
    g2(0)

    def step(st, carry):
        pl.when(st + 2 < nc)(lambda: g1(st + 2))
        pl.when(st + 1 < nc)(lambda: g2(st + 1))

        @pl.when(st < nc)
        def _():
            g3(st)
            compute(st)

        pl.when((st >= 1) & (st < nc + 1))(lambda: r2(st - 1))
        pl.when((st >= 2) & (st < nc + 2))(lambda: r3(st - 2))
        pl.when(st >= 3)(lambda: r4(st - 3))
        return carry

    lax.fori_loop(0, nc + 3, step, 0)

    def drain(c, carry):
        for cp in own_sends(c):
            cp.wait_send()
        for k in (1, 2, 3):
            for cp in z_forwards(c, k):
                cp.wait_send()
        for k in range(4):
            for cp in y_forwards(c, k):
                cp.wait_send()
        for cp in r1_copies(c) + r2_copies(c) + r3_copies(c):
            cp.wait_send()
        return carry

    lax.fori_loop(0, nc, drain, 0)


def solution(mesh):
    def group_step(q_local, k_span, v_span, len_local):
        nb, own, dim = q_local.shape
        span = k_span.shape[1]
        rows = 16 * own
        half, quar = rows // 2, rows // 4
        nc = CHUNKS
        bc = nb // nc
        pitch = bc + 8
        q_planes = jnp.transpose(q_local, (1, 0, 2))
        vm = pltpu.VMEM
        dma = pltpu.SemaphoreType.DMA
        any_spec = pl.BlockSpec(memory_space=pl.ANY)
        out = pl.pallas_call(
            functools.partial(fused, nb, own, span, dim),
            out_shape=jax.ShapeDtypeStruct((own, nb, dim), BF16),
            in_specs=[pl.BlockSpec(memory_space=pltpu.SMEM), any_spec, any_spec, any_spec],
            out_specs=pl.BlockSpec(memory_space=vm),
            scratch_shapes=[
                vm((nb, span, dim), BF16), vm((nb, span, dim), BF16),
                vm((nc, 16, own, bc, dim), BF16),
                vm((rows * pitch, dim), F32), vm((2 * rows * pitch, dim), F32),
                vm((rows, span), jnp.int32), vm((rows, 128), F32), vm((rows, 128), F32),
                vm((nc, half, bc, dim), BF16), vm((nc, half, bc, dim), BF16),
                vm((nc, half, 128), F32), vm((nc, half, 128), F32), vm((nc, half, 128), F32),
                vm((nc, quar, bc, dim), BF16), vm((nc, quar, bc, dim), F32), vm((nc, quar, bc, dim), BF16),
                vm((nc, quar, 128), F32), vm((nc, quar, 128), F32), vm((nc, quar, 128), F32),
                vm((nc, 3, own, bc, dim), BF16), vm((nc, own, bc, dim), F32), vm((nc, 3, own, bc, dim), BF16),
                vm((nc, 3, 4, 128), F32), vm((nc, 4, 128), F32), vm((nc, 3, 4, 128), F32),
                vm((16, 128), F32),
                dma((2, nc)), dma((nc,)), dma((16, nc)), dma((16, nc)), dma((10, nc)), dma((10, nc)),
            ],
            compiler_params=pltpu.CompilerParams(
                collective_id=0, has_side_effects=True, vmem_limit_bytes=67043328),
            name="attend",
        )(len_local, q_planes, k_span, v_span)
        return jnp.transpose(out, (1, 0, 2))

    return jax.shard_map(group_step, mesh=mesh, in_specs=(P("kv", "dup", None), P("kv", "dup", None), P("kv", "dup", None), P("kv")), out_specs=P("kv", "dup", None), check_vma=False)
```

time: 182 us -> 116 us (0.64)
  the two profiles are of different devices: /device:TPU:13 before, /device:TPU:0 now
where the time goes in v1:
time: 116 us
  Pallas kernels  115 us (99%)
  local copies, waits for them, and re-layouts  1.62 us (1%)
    pallas_call x1, Pallas kernels, group_step(): pl.pallas_call(functools.partial(fused, nb, own, span, dim), out_shape=ja...  115 us

profile of v1, /device:TPU:0, one launch (start us, length us, event | category | flops | bytes accessed | tf_op | source)
XLA Modules:
  0.0 116.2 jit_solution(3017567075850637337)
XLA Ops:
  0.0 114.6 %attend.1 = bf16[3,256,128]{2,1,0:T(8,128)(2,1)} custom-call(s32[256]{0:T(256)} %len_ref.1, bf16[3,256,128]{2,1,0:T(8,128)(2,1)} %bitcast.3, bf16[256,256,128]{2,1,0:T(8,128)(2,1)} %k_ref.1, bf16[256,256,128]{2,1,0:T(8,128)(2,1)} %v_ref.1), custom_call_target="tpu_custom_call" | custom-call | tf_op jit(solution)/shard_map/attend/pallas_call | solution.py:281
  114.6 1.6 %copy.6 = bf16[256,3,128]{2,0,1:T(8,128)(2,1)} copy(bf16[256,3,128]{2,0,1:T(8,128)(2,1)} %bitcast.2) | data formatting | bytes 393216

commit v2 on v1

--- a/solution.py
+++ b/solution.py
@@ -10,7 +10,7 @@
 
 DRAFT = 4
 CHUNKS = 8
-UNROLL = 4
+UNROLL = 8
 NEG = -3.4e38
 FLOOR = -3.0e38
 MESH = pl.DeviceIdType.MESH
@@ -19,7 +19,7 @@
 
 
 def fused(nb, own, span, dim, len_ref, q_ref, k_ref, v_ref, out_ref,
-          kbuf, vbuf, qbuf, qf, of, posm, macc, laccs,
+          kbuf, vbuf, qbuf, qf, of, posm, macc, laccs, sbuf, pbuf,
           p1s, p1r, e1s, e1k, e1r, p2s, p2k, p2r, e2s, e2k, e2r, p3s, p3k, p3r, e3s, e3k, e3r,
           wtmp, kvsem, qsem, gs, gr, rs, rr):
     nc = CHUNKS
@@ -138,30 +138,37 @@
         laccs[...] = jnp.ones_like(laccs)
         lanes = lax.broadcasted_iota(jnp.int32, (rows, 128), 1)
 
-        def group(g, carry):
+        def scores(j):
+            qb = qf[pl.ds(j, rows, stride=pitch), :].astype(BF16)
+            sbuf[j] = lax.dot_general(qb, kbuf[c * bc + j], (((1,), (1,)), ((), ())), preferred_element_type=F32)
+
+        def soften(j, mv, lv):
+            s = jnp.where(posm[...] <= len_ref[c * bc + j], sbuf[j], NEG)
+            mx = jnp.maximum(jnp.max(s, axis=1, keepdims=True), FLOOR)
+            p = jnp.exp2((s - mx) * (scale * math.log2(math.e)))
+            pbuf[j] = p.astype(BF16)
+            hit = lanes == j
+            return jnp.where(hit, mx, mv), jnp.where(hit, jnp.sum(p, axis=1, keepdims=True), lv)
+
+        def weigh(j):
+            of[pl.ds(base + j, rows, stride=pitch), :] = jnp.dot(pbuf[j], vbuf[c * bc + j], preferred_element_type=F32)
+
+        def soften_group(g, carry):
             mv, lv = macc[...], laccs[...]
             for u in range(UNROLL):
-                j = g * UNROLL + u
-                b = c * bc + j
-                qb = qf[pl.ds(j, rows, stride=pitch), :].astype(BF16)
-                s = lax.dot_general(qb, kbuf[b], (((1,), (1,)), ((), ())), preferred_element_type=F32)
-                s = jnp.where(posm[...] <= len_ref[b], s, NEG)
-                mx = jnp.maximum(jnp.max(s, axis=1, keepdims=True), FLOOR)
-                p = jnp.exp2((s - mx) * (scale * math.log2(math.e)))
-                den = jnp.maximum(jnp.sum(p, axis=1, keepdims=True), 1.0)
-                o = jnp.dot(p.astype(BF16), vbuf[b], preferred_element_type=F32) * (1.0 / den)
-                of[pl.ds(base + j, rows, stride=pitch), :] = o
-                hit = lanes == j
-                mv = jnp.where(hit, mx, mv)
-                lv = jnp.where(hit, den, lv)
+                mv, lv = soften(g * UNROLL + u, mv, lv)
             macc[...] = mv
             laccs[...] = lv
             return carry
 
-        lax.fori_loop(0, bc // UNROLL, group, 0)
-        lse = macc[...] * scale + jnp.log(laccs[...])
-        e1s[c] = lse[half:]
-        e1k[c] = lse[:half]
+        for j in range(bc):
+            scores(j)
+        lax.fori_loop(0, bc // UNROLL, soften_group, 0)
+        for j in range(bc):
+            weigh(j)
+        mx, den = macc[...] * scale, laccs[...]
+        e1k[c, 0], e1k[c, 1] = mx[:half], den[:half]
+        e1s[c, 0], e1s[c, 1] = mx[half:], den[half:]
         for r in range(half):
             p1s[c, r] = of[pl.ds(base + (half + r) * pitch, bc), :].astype(BF16)
         for cp in r1_copies(c):
@@ -177,14 +184,18 @@
         for cp in r1_copies(c):
             cp.wait_recv()
         base = (c % 2) * (rows * pitch)
-        w, lse = merge(e1k[c], e1r[c])
+        ma, mb = e1k[c, 0], e1r[c, 0]
+        top = jnp.maximum(ma, mb)
+        ea, eb = jnp.exp(ma - top), jnp.exp(mb - top)
+        tot = jnp.maximum(ea * e1k[c, 1] + eb * e1r[c, 1], 1.0)
+        lse = top + jnp.log(tot)
+        inv = 1.0 / tot
         e2k[c] = lse[:quar]
         e2s[c] = lse[quar:]
-        wt = w.T
+        wat, wbt = (ea * inv).T, (eb * inv).T
         for r in list(range(quar, half)) + list(range(quar)):
-            wb = wt[:bc, r:r + 1]
-            o1 = of[pl.ds(base + r * pitch, bc), :]
-            o = (1.0 - wb) * o1 + wb * p1r[c, r].astype(F32)
+            o = (wat[:bc, r:r + 1] * of[pl.ds(base + r * pitch, bc), :]
+                 + wbt[:bc, r:r + 1] * p1r[c, r].astype(F32))
             if r < quar:
                 p2k[c, r] = o
             else:
@@ -287,9 +298,9 @@
                 vm((nb, span, dim), BF16), vm((nb, span, dim), BF16),
                 vm((nc, 16, own, bc, dim), BF16),
                 vm((rows * pitch, dim), F32), vm((2 * rows * pitch, dim), F32),
-                vm((rows, span), jnp.int32), vm((rows, 128), F32), vm((rows, 128), F32),
+                vm((rows, span), jnp.int32), vm((rows, 128), F32), vm((rows, 128), F32), vm((bc, rows, span), F32), vm((bc, rows, span), BF16),
                 vm((nc, half, bc, dim), BF16), vm((nc, half, bc, dim), BF16),
-                vm((nc, half, 128), F32), vm((nc, half, 128), F32), vm((nc, half, 128), F32),
+                vm((nc, 2, half, 128), F32), vm((nc, 2, half, 128), F32), vm((nc, 2, half, 128), F32),
                 vm((nc, quar, bc, dim), BF16), vm((nc, quar, bc, dim), F32), vm((nc, quar, bc, dim), BF16),
                 vm((nc, quar, 128), F32), vm((nc, quar, 128), F32), vm((nc, quar, 128), F32),
                 vm((nc, 3, own, bc, dim), BF16), vm((nc, own, bc, dim), F32), vm((nc, 3, own, bc, dim), BF16),

time: 116 us -> 68.3 us (0.59)
  Pallas kernels: 115 us -> 66.5 us
    pallas_call x1, Pallas kernels: 115 us -> 66.5 us  [group_step(): pl.pallas_call(functools.partial(fused, nb, own, span, dim), out_shape=ja...]
where the time goes in v2:
time: 68.3 us; the launch traced here: 68.2 us
  Pallas kernels  66.5 us (97%)
  local copies, waits for them, and re-layouts  1.62 us (2%)
    pallas_call x1, Pallas kernels, group_step(): pl.pallas_call(functools.partial(fused, nb, own, span, dim), out_shape=ja...  66.5 us
    unnamed x1, local copies, waits for them, and re-layouts  1.62 us

profile of v2, /device:TPU:0, one launch (start us, length us, event | category | flops | bytes accessed | tf_op | source)
XLA Modules:
  0.0 68.2 jit_solution(161023268990329984)
XLA Ops:
  0.0 66.5 %attend.1 = bf16[3,256,128]{2,1,0:T(8,128)(2,1)} custom-call(s32[256]{0:T(256)} %len_ref.1, bf16[3,256,128]{2,1,0:T(8,128)(2,1)} %bitcast.3, bf16[256,256,128]{2,1,0:T(8,128)(2,1)} %k_ref.1, bf16[256,256,128]{2,1,0:T(8,128)(2,1)} %v_ref.1), custom_call_target="tpu_custom_call" | custom-call | tf_op jit(solution)/shard_map/attend/pallas_call | solution.py:292
  66.5 1.6 %copy.6 = bf16[256,3,128]{2,0,1:T(8,128)(2,1)} copy(bf16[256,3,128]{2,0,1:T(8,128)(2,1)} %bitcast.2) | data formatting | bytes 393216

commit v3 on v0

v3 whole, which is shorter than its diff:
```python
import functools
import math

import jax
import jax.numpy as jnp
from jax import lax
from jax.experimental import pallas as pl
from jax.experimental.pallas import tpu as pltpu
from jax.sharding import PartitionSpec as P

CHUNKS = 8
UNROLL = 32
AHEAD = 3
LAG = (0, 1, 3, 4, 5, 7, 9, 11)
B_MOD, B_REM = 100, 50
NEG = -3.4e38
FLOOR = -3.0e38
MESH = pl.DeviceIdType.MESH
F32 = jnp.float32
BF16 = jnp.bfloat16
N_B = len([c for c in range(CHUNKS) if c % B_MOD == B_REM])
N_A = CHUNKS - N_B


def fused(nb, own, span, dim, len_ref, q_ref, k_ref, v_ref, out_ref,
          kbuf, vbuf, qbuf, qf, of, posm, macc, dacc, sbuf, pbuf,
          p1s, p1r, e1k, e1s, e1r, part, lse, ltmp,
          ys, yr, zns, znr, zos, zor, zfs, zfr,
          eys, eyr, ens, enr, eos, eor, efs, efr,
          kvsem, qsem, ss, rq, rr):
    nc = CHUNKS
    bc = nb // nc
    pitch = bc + 8
    rows = 16 * own
    half = rows // 2
    scale = dim ** -0.5
    me = lax.axis_index("dup")
    core, yy, zz = me % 2, (me // 2) % 2, me // 4
    inner = ((zz + 1) // 2) % 2
    partner = me + 1 - 2 * core
    ypeer = me + 2 - 4 * yy
    z1 = me + 4 * (1 - 2 * (zz % 2))
    z2 = me + 4 * (2 - 4 * (zz // 2))
    z3 = me + 4 * (3 - 2 * zz)
    far_inner = me + 4 * (2 - zz // 2 - zz)

    def is_b(c):
        return c % B_MOD == B_REM

    def by_type(c, fn):
        pl.when(is_b(c))(lambda: fn(c, 2))
        pl.when(jnp.logical_not(is_b(c)))(lambda: fn(c, 1))

    def remote(src, dst, ssem, rsem, dev):
        return pltpu.make_async_remote_copy(src_ref=src, dst_ref=dst, send_sem=ssem, recv_sem=rsem,
                                            device_id={"dup": dev}, device_id_type=MESH)

    def send(src, dst, si, rsem, dev):
        remote(src, dst, ss.at[si], rsem, dev).start()

    def recv(ref, rsem):
        remote(ref, ref, ss.at[0], rsem, partner).wait_recv()

    def kv_copies(c):
        sl = pl.ds(c * bc, bc)
        return (pltpu.make_async_copy(k_ref.at[sl], kbuf.at[sl], kvsem.at[c]),
                pltpu.make_async_copy(v_ref.at[sl], vbuf.at[sl], kvsem.at[c]))

    def own_q(c):
        return pltpu.make_async_copy(q_ref.at[:, pl.ds(c * bc, bc)], qbuf.at[c, 0, 0, 0], qsem)

    def start_q(c, carry):
        own_q(c).start()
        return carry

    def start_kv(c, carry):
        for cp in kv_copies(c):
            cp.start()
        return carry

    lax.fori_loop(0, nc, start_q, 0)
    lax.fori_loop(0, nc, start_kv, 0)

    barrier = pltpu.get_barrier_semaphore()
    peers = (partner, ypeer, z1, z2, z3)
    for dev in peers:
        pl.semaphore_signal(barrier, inc=1, device_id={"dup": dev}, device_id_type=MESH)

    rowid = lax.broadcasted_iota(jnp.int32, (rows, span), 0)
    lane = lax.broadcasted_iota(jnp.int32, (rows, span), 1)
    slot = (rowid * 171) >> 9
    item = rowid - 3 * slot
    rel = (slot & 3) * 4 + ((slot >> 2) & 1) * 2 + (slot >> 3)
    tok = (own * (rel ^ me) + item) & 3
    posm[...] = me * span + lane + 4 - tok
    ltmp[...] = jnp.zeros_like(ltmp)

    pltpu.make_async_copy(q_ref, q_ref, qsem).wait()
    pl.semaphore_wait(barrier, len(peers))

    def q_z_own(c, ny):
        y = pl.ds(0, ny)
        src = qbuf.at[c, 0, y, 0]
        send(src, qbuf.at[c, 0, y, 2 + inner], ny - 1, rq.at[1, c], far_inner)
        send(src, qbuf.at[c, 0, y, 1], ny - 1, rq.at[0, c], z1)

    def q_z_relay(c, ny):
        y = pl.ds(0, ny)
        recv(qbuf.at[c, 0, y, pl.ds(2, 2)], rq.at[1, c])

        @pl.when(inner == 1)
        def _():
            send(qbuf.at[c, 0, y, 2], qbuf.at[c, 0, y, 3], 2 + ny - 1, rq.at[1, c], z1)
            send(qbuf.at[c, 0, y, 3], qbuf.at[c, 0, y, 2], 2 + ny - 1, rq.at[1, c], z1)

    def q_z_end(c, ny):
        recv(qbuf.at[c, 0, pl.ds(0, ny), 1], rq.at[0, c])

    def q_y(c, ny):
        if ny == 1:
            z = pl.ds(1, 3)
            send(qbuf.at[c, 0, 0, z], qbuf.at[c, 0, 1, z], 4, rq.at[2, c], ypeer)
        else:
            send(qbuf.at[c, 0, 0, 0], qbuf.at[c, 0, 1, 0], 5, rq.at[2, c], ypeer)

    def q_y_wait(c, ny):
        recv(qbuf.at[c, 0, 1] if ny == 1 else qbuf.at[c, 0, 1, 0], rq.at[2, c])

    def q0(c, ny):
        if ny == 1:
            q_z_own(c, ny)
            send(qbuf.at[c, 0, 0, 0], qbuf.at[c, 0, 1, 0], 4, rq.at[2, c], ypeer)
        else:
            q_y(c, ny)

    def q1(c, ny):
        if ny == 1:
            pl.when(inner == 1)(lambda: q_z_relay(c, ny))
        else:
            q_y_wait(c, ny)
            q_z_own(c, ny)

    def q2(c, ny):
        if ny == 1:
            q_z_end(c, ny)
            pl.when(inner == 0)(lambda: q_z_relay(c, ny))
            q_y(c, ny)
        else:
            pl.when(inner == 1)(lambda: q_z_relay(c, ny))

    def q3(c, ny):
        if ny == 1:
            q_y_wait(c, ny)
        else:
            q_z_end(c, ny)
            pl.when(inner == 0)(lambda: q_z_relay(c, ny))

    def q_partner(c):
        send(qbuf.at[c, 0], qbuf.at[c, 1], 6, rq.at[3, c], partner)

    def compute(c):
        recv(qbuf.at[c, 1], rq.at[3, c])
        for s in range(16):
            for i in range(own):
                qf[pl.ds((s * own + i) * pitch, bc), :] = qbuf[c, s // 8, (s // 4) % 2, s % 4, i].astype(F32)
        pltpu.make_async_copy(k_ref.at[pl.ds(0, 2 * bc)], kbuf.at[pl.ds(0, 2 * bc)], kvsem.at[c]).wait()
        base = (c % 2) * (rows * pitch)
        macc[...] = jnp.zeros_like(macc)
        dacc[...] = jnp.zeros_like(dacc)
        place = lax.broadcasted_iota(jnp.int32, (rows, 128), 1)
        rid = lax.broadcasted_iota(jnp.int32, (rows, 128), 0)
        place = place - bc * (rid - 3 * ((rid * 171) >> 9))

        def scores(j):
            qb = qf[pl.ds(j, rows, stride=pitch), :].astype(BF16)
            sbuf[j] = lax.dot_general(qb, kbuf[c * bc + j], (((1,), (1,)), ((), ())), preferred_element_type=F32)

        def soften(j, mv, dv):
            s = jnp.where(posm[...] <= len_ref[c * bc + j], sbuf[j], NEG)
            mx = jnp.maximum(jnp.max(s, axis=1, keepdims=True), FLOOR)
            p = jnp.exp2((s - mx) * (scale * math.log2(math.e)))
            pbuf[j] = p.astype(BF16)
            hit = place == j
            return jnp.where(hit, mx, mv), jnp.where(hit, jnp.sum(p, axis=1, keepdims=True), dv)

        def soften_group(g, carry):
            mv, dv = macc[...], dacc[...]
            for u in range(UNROLL):
                mv, dv = soften(g * UNROLL + u, mv, dv)
            macc[...] = mv
            dacc[...] = dv
            return carry

        for j in range(bc):
            scores(j)
        lax.fori_loop(0, bc // UNROLL, soften_group, 0)
        for j in range(bc):
            of[pl.ds(base + j, rows, stride=pitch), :] = jnp.dot(pbuf[j], vbuf[c * bc + j], preferred_element_type=F32)
        for t, acc in ((0, macc), (1, dacc)):
            line = acc[pl.ds(0, 16, stride=3), :] + acc[pl.ds(1, 16, stride=3), :] + acc[pl.ds(2, 16, stride=3), :]
            if t == 0:
                line = line * scale
            e1k[c, t] = line[:8]
            e1s[c, t] = line[8:]
        for r in range(half):
            p1s[c, r] = of[pl.ds(base + (half + r) * pitch, bc), :].astype(BF16)
        send(e1s.at[c], e1r.at[c], 8, rr.at[1, c], partner)
        send(p1s.at[c], p1r.at[c], 7, rr.at[0, c], partner)

    def cut(w, line, i):
        return w[i * bc:(i + 1) * bc, line:line + 1]

    def lines(refs):
        for n, ref in refs:
            ltmp[n:n + 1] = ref
        return ltmp[...]

    def weights(*ls):
        top = functools.reduce(jnp.maximum, ls)
        es = [jnp.exp(x - top) for x in ls]
        tot = functools.reduce(lambda a, b: a + b, es)
        inv = 1.0 / tot
        return [(e * inv).T for e in es], top + jnp.log(tot)

    def merge_partner(c):
        recv(e1r.at[c], rr.at[1, c])
        ma, mb = e1k[c, 0], e1r[c, 0]
        top = jnp.maximum(ma, mb)
        ea, eb = jnp.exp(ma - top), jnp.exp(mb - top)
        tot = jnp.maximum(ea * e1k[c, 1] + eb * e1r[c, 1], 1.0)
        inv = 1.0 / tot
        lse[c] = top + jnp.log(tot)
        wa, wb = (ea * inv).T, (eb * inv).T
        recv(p1r.at[c], rr.at[0, c])
        base = (c % 2) * (rows * pitch)
        for n in range(8):
            for i in range(own):
                r = n * own + i
                part[c, n, i] = (cut(wa, n, i) * of[pl.ds(base + r * pitch, bc), :]
                                 + cut(wb, n, i) * p1r[c, r].astype(F32))

    def y_send(c, ny):
        for z in range(4 if ny == 1 else 1):
            eys[c, z] = lse[c, 4 + z:5 + z]
            for i in range(own):
                ys[c, z, i] = part[c, 4 + z, i].astype(BF16)
        if ny == 1:
            send(eys.at[c], eyr.at[c], 10, rr.at[3, c], ypeer)
            send(ys.at[c], yr.at[c], 9, rr.at[2, c], ypeer)
        else:
            send(eys.at[c, 0], eyr.at[c, 0], 12, rr.at[3, c], ypeer)
            send(ys.at[c, 0], yr.at[c, 0], 11, rr.at[2, c], ypeer)

    def y_merge(c, ny):
        if ny == 1:
            recv(eyr.at[c], rr.at[3, c])
            (wa, wb), new = weights(lse[c], lines([(z, eyr[c, z]) for z in range(4)]))
            lse[c] = new
            recv(yr.at[c], rr.at[2, c])
            for z in range(4):
                for i in range(own):
                    part[c, z, i] = cut(wa, z, i) * part[c, z, i] + cut(wb, z, i) * yr[c, z, i].astype(F32)
        else:
            recv(eyr.at[c, 0], rr.at[3, c])
            (wa, wb), _ = weights(lse[c], lines([(0, eyr[c, 0])]))
            recv(yr.at[c, 0], rr.at[2, c])
            for i in range(own):
                o = cut(wa, 0, i) * part[c, 0, i] + cut(wb, 0, i) * yr[c, 0, i].astype(F32)
                out_ref[i, pl.ds(c * bc, bc)] = o.astype(BF16)

    def z_send(c, ny):
        y = pl.ds(0, ny)

        @pl.when(inner == 0)
        def _():
            for m in range(2):
                for h in range(ny):
                    eos[c, m, h] = lse[c, 4 * h + 2 + m:4 * h + 3 + m]
                    for i in range(own):
                        zos[c, m, h, i] = part[c, 4 * h + 2 + m, i].astype(BF16)
            send(eos.at[c, :, y], eor.at[c, :, y], 18 + 2 * (ny - 1), rr.at[7, c], z1)
            send(zos.at[c, :, y], zor.at[c, :, y], 17 + 2 * (ny - 1), rr.at[6, c], z1)

        for h in range(ny):
            ens[c, h] = lse[c, 4 * h + 1:4 * h + 2]
            for i in range(own):
                zns[c, h, i] = part[c, 4 * h + 1, i].astype(BF16)
        send(ens.at[c, y], enr.at[c, y], 14 + 2 * (ny - 1), rr.at[5, c], z1)
        send(zns.at[c, y], znr.at[c, y], 13 + 2 * (ny - 1), rr.at[4, c], z1)

    def z_relay(c, ny):
        y = pl.ds(0, ny)
        recv(eor.at[c, :, y], rr.at[7, c])
        (wa, wb), new = weights(lse[c], lines([(4 * h + 3 - m, eor[c, m, h]) for m in range(2) for h in range(ny)]))
        recv(zor.at[c, :, y], rr.at[6, c])
        for m in range(2):
            for h in range(ny):
                n = 4 * h + 3 - m
                efs[c, m, h] = new[n:n + 1]
                for i in range(own):
                    o = cut(wa, n, i) * part[c, n, i] + cut(wb, n, i) * zor[c, m, h, i].astype(F32)
                    zfs[c, m, h, i] = o.astype(BF16)
        for m, dev in ((1, z2), (0, z3)):
            send(efs.at[c, m, y], efr.at[c, y], 22 + 2 * (ny - 1), rr.at[9, c], dev)
            send(zfs.at[c, m, y], zfr.at[c, y], 21 + 2 * (ny - 1), rr.at[8, c], dev)

    def z_merge(c, ny):
        y = pl.ds(0, ny)
        recv(enr.at[c, y], rr.at[5, c])
        recv(efr.at[c, y], rr.at[9, c])
        near = lines([(4 * h, enr[c, h]) for h in range(ny)])
        far = lines([(4 * h, efr[c, h]) for h in range(ny)])
        (wa, wb, wc), new = weights(lse[c], near, far)
        lse[c] = new
        recv(znr.at[c, y], rr.at[4, c])
        recv(zfr.at[c, y], rr.at[8, c])
        for h in range(ny):
            n = 4 * h
            for i in range(own):
                o = (cut(wa, n, i) * part[c, n, i] + cut(wb, n, i) * znr[c, h, i].astype(F32)
                     + cut(wc, n, i) * zfr[c, h, i].astype(F32))
                if ny == 1:
                    out_ref[i, pl.ds(c * bc, bc)] = o.astype(BF16)
                else:
                    part[c, n, i] = o

    def r0(c):
        merge_partner(c)
        by_type(c, lambda c, ny: y_send(c, ny) if ny == 1 else z_send(c, ny))

    def r1(c, ny):
        if ny == 1:
            y_merge(c, ny)
            z_send(c, ny)
        else:
            pl.when(inner == 1)(lambda: z_relay(c, ny))

    def r2(c, ny):
        if ny == 1:
            pl.when(inner == 1)(lambda: z_relay(c, ny))
        else:
            z_merge(c, ny)
            y_send(c, ny)

    def r3(c, ny):
        if ny == 1:
            z_merge(c, ny)
        else:
            y_merge(c, ny)

    def at(c, fn):
        pl.when((c >= 0) & (c < nc))(lambda: fn(c))

    def typed(fn):
        return lambda c: by_type(c, fn)

    def first(c, carry):
        by_type(c, q0)
        return carry

    lax.fori_loop(0, AHEAD, first, 0)

    def step(st, carry):
        at(st + AHEAD, typed(q0))
        at(st - LAG[0], typed(q1))
        at(st - LAG[1], typed(q2))

        @pl.when((st >= LAG[2]) & (st - LAG[2] < nc))
        def _():
            by_type(st - LAG[2], q3)
            q_partner(st - LAG[2])

        at(st - LAG[3], compute)
        at(st - LAG[4], r0)
        at(st - LAG[5], typed(r1))
        at(st - LAG[6], typed(r2))
        at(st - LAG[7], typed(r3))
        return carry

    lax.fori_loop(0, nc + LAG[7], step, 0)

    def sent(ref, si):
        remote(ref, ref, ss.at[si], rq.at[0, 0], partner).wait_send()

    for t, n in ((0, N_A), (1, N_B)):
        if n == 0:
            continue
        c, y = pl.ds(0, n), pl.ds(0, t + 1)
        sent(qbuf.at[c, 0, y, pl.ds(0, 2)], t)
        sent(qbuf.at[c, 0, 0] if t == 0 else qbuf.at[c, 0, 0, 0], 4 + t)
        sent(ys.at[c] if t == 0 else ys.at[c, 0], 9 + 2 * t)
        sent(eys.at[c] if t == 0 else eys.at[c, 0], 10 + 2 * t)
        sent(zns.at[c, y], 13 + 2 * t)
        sent(ens.at[c, y], 14 + 2 * t)

        @pl.when(inner == 0)
        def _():
            sent(zos.at[c, :, y], 17 + 2 * t)
            sent(eos.at[c, :, y], 18 + 2 * t)

        @pl.when(inner == 1)
        def _():
            sent(qbuf.at[c, 0, y, pl.ds(0, 2)], 2 + t)
            sent(zfs.at[c, :, y], 21 + 2 * t)
            sent(efs.at[c, :, y], 22 + 2 * t)

    sent(qbuf.at[:, 0], 6)
    sent(p1s, 7)
    sent(e1s, 8)


def solution(mesh):
    def group_step(q_local, k_span, v_span, len_local):
        nb, own, dim = q_local.shape
        span = k_span.shape[1]
        rows = 16 * own
        half = rows // 2
        nc = CHUNKS
        bc = nb // nc
        pitch = bc + 8
        q_planes = jnp.transpose(q_local, (1, 0, 2))
        vm = pltpu.VMEM
        dma = pltpu.SemaphoreType.DMA
        any_spec = pl.BlockSpec(memory_space=pl.ANY)

        def blocks(*lead):
            return vm((nc, *lead, own, bc, dim), BF16)

        def line(*lead):
            return vm((nc, *lead, 1, 128), F32)

        out = pl.pallas_call(
            functools.partial(fused, nb, own, span, dim),
            out_shape=jax.ShapeDtypeStruct((own, nb, dim), BF16),
            in_specs=[pl.BlockSpec(memory_space=pltpu.SMEM), any_spec, any_spec, any_spec],
            out_specs=pl.BlockSpec(memory_space=vm),
            scratch_shapes=[
                vm((nb, span, dim), BF16), vm((nb, span, dim), BF16),
                blocks(2, 2, 4),
                vm((rows * pitch, dim), F32), vm((2 * rows * pitch, dim), F32),
                vm((rows, span), jnp.int32), vm((rows, 128), F32), vm((rows, 128), F32),
                vm((bc, rows, span), F32), vm((bc, rows, span), BF16),
                vm((nc, half, bc, dim), BF16), vm((nc, half, bc, dim), BF16),
                vm((nc, 2, 8, 128), F32), vm((nc, 2, 8, 128), F32), vm((nc, 2, 8, 128), F32),
                vm((nc, 8, own, bc, dim), F32), vm((nc, 8, 128), F32), vm((8, 128), F32),
                blocks(4), blocks(4), blocks(2), blocks(2),
                blocks(2, 2), blocks(2, 2), blocks(2, 2), blocks(2),
                line(4), line(4), line(2), line(2), line(2, 2), line(2, 2), line(2, 2), line(2),
                dma((nc,)), dma, dma((25,)), dma((4, nc)), dma((10, nc)),
            ],
            compiler_params=pltpu.CompilerParams(
                collective_id=0, has_side_effects=True, vmem_limit_bytes=67043328),
            name="attend",
        )(len_local, q_planes, k_span, v_span)
        return jnp.transpose(out, (1, 0, 2))

    return jax.shard_map(group_step, mesh=mesh, in_specs=(P("kv", "dup", None), P("kv", "dup", None), P("kv", "dup", None), P("kv")), out_specs=P("kv", "dup", None), check_vma=False)
```

time: 182 us -> 56.3 us (0.31)
  the two profiles are of different devices: /device:TPU:13 before, /device:TPU:0 now
where the time goes in v3:
time: 56.3 us; the launch traced here: 56.1 us
  Pallas kernels  54.5 us (97%)
  local copies, waits for them, and re-layouts  1.62 us (3%)
    pallas_call x1, Pallas kernels, group_step(): pl.pallas_call(functools.partial(fused, nb, own, span, dim), out_shape=ja...  54.5 us
    unnamed x1, local copies, waits for them, and re-layouts  1.62 us

profile of v3, /device:TPU:0, one launch (start us, length us, event | category | flops | bytes accessed | tf_op | source)
XLA Modules:
  0.0 56.1 jit_solution(10765198497821077569)
XLA Ops:
  0.0 54.5 %attend.1 = bf16[3,256,128]{2,1,0:T(8,128)(2,1)} custom-call(s32[256]{0:T(256)} %len_ref.1, bf16[3,256,128]{2,1,0:T(8,128)(2,1)} %bitcast.3, bf16[256,256,128]{2,1,0:T(8,128)(2,1)} %k_ref.1, bf16[256,256,128]{2,1,0:T(8,128)(2,1)} %v_ref.1), custom_call_target="tpu_custom_call" | custom-call | tf_op jit(solution)/shard_map/attend/pallas_call | solution.py:432
  54.5 1.6 %copy.6 = bf16[256,3,128]{2,0,1:T(8,128)(2,1)} copy(bf16[256,3,128]{2,0,1:T(8,128)(2,1)} %bitcast.2) | data formatting | bytes 393216

commit v4 on v3

--- a/solution.py
+++ b/solution.py
@@ -10,24 +10,22 @@
 
 CHUNKS = 8
 UNROLL = 32
-AHEAD = 3
+AHEAD = 2
+Y_AHEAD = 3
 LAG = (0, 1, 3, 4, 5, 7, 9, 11)
-B_MOD, B_REM = 100, 50
+Q_WAY = "AAABAABA"
+O_WAY = "DDBDDDDD"
 NEG = -3.4e38
 FLOOR = -3.0e38
 MESH = pl.DeviceIdType.MESH
 F32 = jnp.float32
 BF16 = jnp.bfloat16
-N_B = len([c for c in range(CHUNKS) if c % B_MOD == B_REM])
-N_A = CHUNKS - N_B
-
-
 def fused(nb, own, span, dim, len_ref, q_ref, k_ref, v_ref, out_ref,
           kbuf, vbuf, qbuf, qf, of, posm, macc, dacc, sbuf, pbuf,
           p1s, p1r, e1k, e1s, e1r, part, lse, ltmp,
           ys, yr, zns, znr, zos, zor, zfs, zfr,
           eys, eyr, ens, enr, eos, eor, efs, efr,
-          kvsem, qsem, ss, rq, rr):
+          obuf, kvsem, qsem, osem, ss, rq, rr):
     nc = CHUNKS
     bc = nb // nc
     pitch = bc + 8
@@ -44,12 +42,19 @@
     z3 = me + 4 * (3 - 2 * zz)
     far_inner = me + 4 * (2 - zz // 2 - zz)
 
-    def is_b(c):
-        return c % B_MOD == B_REM
-
-    def by_type(c, fn):
-        pl.when(is_b(c))(lambda: fn(c, 2))
-        pl.when(jnp.logical_not(is_b(c)))(lambda: fn(c, 1))
+    def upto(n):
+        return pl.ds(0, n)
+
+    def among(c, ways, way):
+        hits = [c == k for k in range(nc) if ways[k] == way]
+        return functools.reduce(jnp.logical_or, hits, jnp.bool_(False))
+
+    def by_way(ways, fns):
+        def run(c):
+            for way, fn in fns.items():
+                if fn is not None and way in ways:
+                    pl.when(among(c, ways, way))(functools.partial(fn, c))
+        return run
 
     def remote(src, dst, ssem, rsem, dev):
         return pltpu.make_async_remote_copy(src_ref=src, dst_ref=dst, send_sem=ssem, recv_sem=rsem,
@@ -98,65 +103,62 @@
     pltpu.make_async_copy(q_ref, q_ref, qsem).wait()
     pl.semaphore_wait(barrier, len(peers))
 
-    def q_z_own(c, ny):
-        y = pl.ds(0, ny)
-        src = qbuf.at[c, 0, y, 0]
-        send(src, qbuf.at[c, 0, y, 2 + inner], ny - 1, rq.at[1, c], far_inner)
-        send(src, qbuf.at[c, 0, y, 1], ny - 1, rq.at[0, c], z1)
-
-    def q_z_relay(c, ny):
-        y = pl.ds(0, ny)
-        recv(qbuf.at[c, 0, y, pl.ds(2, 2)], rq.at[1, c])
-
+    def q_far(c, ny):
+        y = upto(ny)
+        send(qbuf.at[c, 0, y, 0], qbuf.at[c, 0, y, 2 + inner], ny + ny - 1, rq.at[1, c], far_inner)
+        pl.when(inner == 0)(lambda: q_near(c, ny))
+
+    def q_near(c, ny):
+        y = upto(ny)
+        send(qbuf.at[c, 0, y, 0], qbuf.at[c, 0, y, 1], ny + ny - 1, rq.at[0, c], z1)
+
+    def q_relayed(c, ny):
+        recv(qbuf.at[c, 0, upto(ny), pl.ds(2, 2)], rq.at[1, c])
+
+    def q_relay(c, ny):
         @pl.when(inner == 1)
         def _():
-            send(qbuf.at[c, 0, y, 2], qbuf.at[c, 0, y, 3], 2 + ny - 1, rq.at[1, c], z1)
-            send(qbuf.at[c, 0, y, 3], qbuf.at[c, 0, y, 2], 2 + ny - 1, rq.at[1, c], z1)
-
-    def q_z_end(c, ny):
-        recv(qbuf.at[c, 0, pl.ds(0, ny), 1], rq.at[0, c])
-
-    def q_y(c, ny):
-        if ny == 1:
-            z = pl.ds(1, 3)
-            send(qbuf.at[c, 0, 0, z], qbuf.at[c, 0, 1, z], 4, rq.at[2, c], ypeer)
-        else:
-            send(qbuf.at[c, 0, 0, 0], qbuf.at[c, 0, 1, 0], 5, rq.at[2, c], ypeer)
-
-    def q_y_wait(c, ny):
-        recv(qbuf.at[c, 0, 1] if ny == 1 else qbuf.at[c, 0, 1, 0], rq.at[2, c])
-
-    def q0(c, ny):
-        if ny == 1:
-            q_z_own(c, ny)
-            send(qbuf.at[c, 0, 0, 0], qbuf.at[c, 0, 1, 0], 4, rq.at[2, c], ypeer)
-        else:
-            q_y(c, ny)
-
-    def q1(c, ny):
-        if ny == 1:
-            pl.when(inner == 1)(lambda: q_z_relay(c, ny))
-        else:
-            q_y_wait(c, ny)
-            q_z_own(c, ny)
-
-    def q2(c, ny):
-        if ny == 1:
-            q_z_end(c, ny)
-            pl.when(inner == 0)(lambda: q_z_relay(c, ny))
-            q_y(c, ny)
-        else:
-            pl.when(inner == 1)(lambda: q_z_relay(c, ny))
-
-    def q3(c, ny):
-        if ny == 1:
-            q_y_wait(c, ny)
-        else:
-            q_z_end(c, ny)
-            pl.when(inner == 0)(lambda: q_z_relay(c, ny))
+            y = upto(ny)
+            q_relayed(c, ny)
+            send(qbuf.at[c, 0, y, 2], qbuf.at[c, 0, y, 3], 2 * ny, rq.at[1, c], z1)
+            send(qbuf.at[c, 0, y, 3], qbuf.at[c, 0, y, 2], 2 * ny, rq.at[1, c], z1)
+            q_near(c, ny)
+
+    def q_end(c, ny):
+        pl.when(inner == 0)(lambda: q_relayed(c, ny))
+        recv(qbuf.at[c, 0, upto(ny), 1], rq.at[0, c])
+
+    def q_y_own(c, si=5):
+        send(qbuf.at[c, 0, 0, 0], qbuf.at[c, 0, 1, 0], si, rq.at[2, c], ypeer)
+
+    def q_y_rest(c):
+        z = pl.ds(1, 3)
+        send(qbuf.at[c, 0, 0, z], qbuf.at[c, 0, 1, z], 5, rq.at[2, c], ypeer)
 
     def q_partner(c):
-        send(qbuf.at[c, 0], qbuf.at[c, 1], 6, rq.at[3, c], partner)
+        send(qbuf.at[c, 0], qbuf.at[c, 1], 7, rq.at[3, c], partner)
+
+    def q_last(c):
+        recv(qbuf.at[c, 0, 1], rq.at[2, c])
+        q_partner(c)
+
+    def both(*fns):
+        def run(c):
+            for fn in fns:
+                fn(c)
+        return run
+
+    y_own = by_way(Q_WAY, {"A": q_y_own, "B": lambda c: q_y_own(c, 6)})
+    q0 = by_way(Q_WAY, {"A": lambda c: q_far(c, 1)})
+    q1 = by_way(Q_WAY, {
+        "A": lambda c: q_relay(c, 1),
+        "B": both(lambda c: recv(qbuf.at[c, 0, 1, 0], rq.at[2, c]), lambda c: q_far(c, 2))})
+    q2 = by_way(Q_WAY, {
+        "A": both(lambda c: q_end(c, 1), q_y_rest),
+        "B": lambda c: q_relay(c, 2)})
+    q3 = by_way(Q_WAY, {
+        "A": q_last,
+        "B": both(lambda c: q_end(c, 2), q_partner)})
 
     def compute(c):
         recv(qbuf.at[c, 1], rq.at[3, c])
@@ -204,8 +206,14 @@
             e1s[c, t] = line[8:]
         for r in range(half):
             p1s[c, r] = of[pl.ds(base + (half + r) * pitch, bc), :].astype(BF16)
-        send(e1s.at[c], e1r.at[c], 8, rr.at[1, c], partner)
-        send(p1s.at[c], p1r.at[c], 7, rr.at[0, c], partner)
+        send(e1s.at[c], e1r.at[c], 9, rr.at[1, c], partner)
+        send(p1s.at[c], p1r.at[c], 8, rr.at[0, c], partner)
+
+    def finish(c, i, o):
+        obuf[c, i] = o.astype(BF16)
+
+    def ship(c):
+        pltpu.make_async_copy(obuf.at[c], out_ref.at[:, pl.ds(c * bc, bc)], osem).start()
 
     def cut(w, line, i):
         return w[i * bc:(i + 1) * bc, line:line + 1]
@@ -245,11 +253,11 @@
             for i in range(own):
                 ys[c, z, i] = part[c, 4 + z, i].astype(BF16)
         if ny == 1:
-            send(eys.at[c], eyr.at[c], 10, rr.at[3, c], ypeer)
-            send(ys.at[c], yr.at[c], 9, rr.at[2, c], ypeer)
+            send(eys.at[c], eyr.at[c], 11, rr.at[3, c], ypeer)
+            send(ys.at[c], yr.at[c], 10, rr.at[2, c], ypeer)
         else:
-            send(eys.at[c, 0], eyr.at[c, 0], 12, rr.at[3, c], ypeer)
-            send(ys.at[c, 0], yr.at[c, 0], 11, rr.at[2, c], ypeer)
+            send(eys.at[c, 0], eyr.at[c, 0], 13, rr.at[3, c], ypeer)
+            send(ys.at[c, 0], yr.at[c, 0], 12, rr.at[2, c], ypeer)
 
     def y_merge(c, ny):
         if ny == 1:
@@ -265,11 +273,11 @@
             (wa, wb), _ = weights(lse[c], lines([(0, eyr[c, 0])]))
             recv(yr.at[c, 0], rr.at[2, c])
             for i in range(own):
-                o = cut(wa, 0, i) * part[c, 0, i] + cut(wb, 0, i) * yr[c, 0, i].astype(F32)
-                out_ref[i, pl.ds(c * bc, bc)] = o.astype(BF16)
+                finish(c, i, cut(wa, 0, i) * part[c, 0, i] + cut(wb, 0, i) * yr[c, 0, i].astype(F32))
+            ship(c)
 
     def z_send(c, ny):
-        y = pl.ds(0, ny)
+        y = upto(ny)
 
         @pl.when(inner == 0)
         def _():
@@ -278,18 +286,44 @@
                     eos[c, m, h] = lse[c, 4 * h + 2 + m:4 * h + 3 + m]
                     for i in range(own):
                         zos[c, m, h, i] = part[c, 4 * h + 2 + m, i].astype(BF16)
-            send(eos.at[c, :, y], eor.at[c, :, y], 18 + 2 * (ny - 1), rr.at[7, c], z1)
-            send(zos.at[c, :, y], zor.at[c, :, y], 17 + 2 * (ny - 1), rr.at[6, c], z1)
+            send(eos.at[c, :, y], eor.at[c, :, y], 17 + ny + ny, rr.at[7, c], z1)
+            send(zos.at[c, :, y], zor.at[c, :, y], 16 + ny + ny, rr.at[6, c], z1)
 
         for h in range(ny):
             ens[c, h] = lse[c, 4 * h + 1:4 * h + 2]
             for i in range(own):
                 zns[c, h, i] = part[c, 4 * h + 1, i].astype(BF16)
-        send(ens.at[c, y], enr.at[c, y], 14 + 2 * (ny - 1), rr.at[5, c], z1)
-        send(zns.at[c, y], znr.at[c, y], 13 + 2 * (ny - 1), rr.at[4, c], z1)
+        send(ens.at[c, y], enr.at[c, y], 13 + ny + ny, rr.at[5, c], z1)
+        send(zns.at[c, y], znr.at[c, y], 12 + ny + ny, rr.at[4, c], z1)
+
+    def z_send_direct(c):
+        for k, dat, lin in ((2, zos.at[c, 0, 0], eos.at[c, 0, 0]), (3, zos.at[c, 1, 0], eos.at[c, 1, 0]),
+                            (1, zns.at[c, 0], ens.at[c, 0])):
+            lin[...] = lse[c, k:k + 1]
+            for i in range(own):
+                dat[i] = part[c, k, i].astype(BF16)
+        for m, dev in ((1, z3), (0, z2)):
+            send(eos.at[c, m, 0], eor.at[c, m, 0], 19, rr.at[7, c], dev)
+            send(zos.at[c, m, 0], zor.at[c, m, 0], 18, rr.at[6, c], dev)
+        send(ens.at[c, 0], enr.at[c, 0], 15, rr.at[5, c], z1)
+        send(zns.at[c, 0], znr.at[c, 0], 14, rr.at[4, c], z1)
+
+    def z_merge_direct(c):
+        recv(enr.at[c, 0], rr.at[5, c])
+        recv(eor.at[c, :, 0], rr.at[7, c])
+        ls = [lines([(0, ref)]) for ref in (enr[c, 0], eor[c, 0, 0], eor[c, 1, 0])]
+        ws, _ = weights(lse[c], *ls)
+        recv(znr.at[c, 0], rr.at[4, c])
+        recv(zor.at[c, :, 0], rr.at[6, c])
+        for i in range(own):
+            o = cut(ws[0], 0, i) * part[c, 0, i]
+            for w, dat in zip(ws[1:], (znr.at[c, 0], zor.at[c, 0, 0], zor.at[c, 1, 0])):
+                o = o + cut(w, 0, i) * dat[i].astype(F32)
+            finish(c, i, o)
+        ship(c)
 
     def z_relay(c, ny):
-        y = pl.ds(0, ny)
+        y = upto(ny)
         recv(eor.at[c, :, y], rr.at[7, c])
         (wa, wb), new = weights(lse[c], lines([(4 * h + 3 - m, eor[c, m, h]) for m in range(2) for h in range(ny)]))
         recv(zor.at[c, :, y], rr.at[6, c])
@@ -301,11 +335,11 @@
                     o = cut(wa, n, i) * part[c, n, i] + cut(wb, n, i) * zor[c, m, h, i].astype(F32)
                     zfs[c, m, h, i] = o.astype(BF16)
         for m, dev in ((1, z2), (0, z3)):
-            send(efs.at[c, m, y], efr.at[c, y], 22 + 2 * (ny - 1), rr.at[9, c], dev)
-            send(zfs.at[c, m, y], zfr.at[c, y], 21 + 2 * (ny - 1), rr.at[8, c], dev)
+            send(efs.at[c, m, y], efr.at[c, y], 21 + ny + ny, rr.at[9, c], dev)
+            send(zfs.at[c, m, y], zfr.at[c, y], 20 + ny + ny, rr.at[8, c], dev)
 
     def z_merge(c, ny):
-        y = pl.ds(0, ny)
+        y = upto(ny)
         recv(enr.at[c, y], rr.at[5, c])
         recv(efr.at[c, y], rr.at[9, c])
         near = lines([(4 * h, enr[c, h]) for h in range(ny)])
@@ -320,61 +354,55 @@
                 o = (cut(wa, n, i) * part[c, n, i] + cut(wb, n, i) * znr[c, h, i].astype(F32)
                      + cut(wc, n, i) * zfr[c, h, i].astype(F32))
                 if ny == 1:
-                    out_ref[i, pl.ds(c * bc, bc)] = o.astype(BF16)
+                    finish(c, i, o)
                 else:
                     part[c, n, i] = o
+        if ny == 1:
+            ship(c)
+
+    r0_send = by_way(O_WAY, {"D": lambda c: y_send(c, 1), "A": lambda c: y_send(c, 1), "B": lambda c: z_send(c, 2)})
 
     def r0(c):
         merge_partner(c)
-        by_type(c, lambda c, ny: y_send(c, ny) if ny == 1 else z_send(c, ny))
-
-    def r1(c, ny):
-        if ny == 1:
-            y_merge(c, ny)
-            z_send(c, ny)
-        else:
-            pl.when(inner == 1)(lambda: z_relay(c, ny))
-
-    def r2(c, ny):
-        if ny == 1:
-            pl.when(inner == 1)(lambda: z_relay(c, ny))
-        else:
-            z_merge(c, ny)
-            y_send(c, ny)
-
-    def r3(c, ny):
-        if ny == 1:
-            z_merge(c, ny)
-        else:
-            y_merge(c, ny)
+        r0_send(c)
+
+    def relay(c, ny):
+        pl.when(inner == 1)(lambda: z_relay(c, ny))
+
+    r1 = by_way(O_WAY, {
+        "D": both(lambda c: y_merge(c, 1), z_send_direct),
+        "A": both(lambda c: y_merge(c, 1), lambda c: z_send(c, 1)),
+        "B": lambda c: relay(c, 2)})
+    r2 = by_way(O_WAY, {
+        "D": None,
+        "A": lambda c: relay(c, 1),
+        "B": both(lambda c: z_merge(c, 2), lambda c: y_send(c, 2))})
+    r3 = by_way(O_WAY, {
+        "D": z_merge_direct,
+        "A": lambda c: z_merge(c, 1),
+        "B": lambda c: y_merge(c, 2)})
 
     def at(c, fn):
         pl.when((c >= 0) & (c < nc))(lambda: fn(c))
 
-    def typed(fn):
-        return lambda c: by_type(c, fn)
-
     def first(c, carry):
-        by_type(c, q0)
+        pl.when(c < AHEAD)(lambda: q0(c))
+        y_own(c)
         return carry
 
-    lax.fori_loop(0, AHEAD, first, 0)
+    lax.fori_loop(0, Y_AHEAD, first, 0)
 
     def step(st, carry):
-        at(st + AHEAD, typed(q0))
-        at(st - LAG[0], typed(q1))
-        at(st - LAG[1], typed(q2))
-
-        @pl.when((st >= LAG[2]) & (st - LAG[2] < nc))
-        def _():
-            by_type(st - LAG[2], q3)
-            q_partner(st - LAG[2])
-
+        at(st + AHEAD, q0)
+        at(st + Y_AHEAD, y_own)
+        at(st - LAG[0], q1)
+        at(st - LAG[1], q2)
+        at(st - LAG[2], q3)
         at(st - LAG[3], compute)
         at(st - LAG[4], r0)
-        at(st - LAG[5], typed(r1))
-        at(st - LAG[6], typed(r2))
-        at(st - LAG[7], typed(r3))
+        at(st - LAG[5], r1)
+        at(st - LAG[6], r2)
+        at(st - LAG[7], r3)
         return carry
 
     lax.fori_loop(0, nc + LAG[7], step, 0)
@@ -382,31 +410,42 @@
     def sent(ref, si):
         remote(ref, ref, ss.at[si], rq.at[0, 0], partner).wait_send()
 
-    for t, n in ((0, N_A), (1, N_B)):
-        if n == 0:
-            continue
-        c, y = pl.ds(0, n), pl.ds(0, t + 1)
-        sent(qbuf.at[c, 0, y, pl.ds(0, 2)], t)
-        sent(qbuf.at[c, 0, 0] if t == 0 else qbuf.at[c, 0, 0, 0], 4 + t)
-        sent(ys.at[c] if t == 0 else ys.at[c, 0], 9 + 2 * t)
-        sent(eys.at[c] if t == 0 else eys.at[c, 0], 10 + 2 * t)
-        sent(zns.at[c, y], 13 + 2 * t)
-        sent(ens.at[c, y], 14 + 2 * t)
-
-        @pl.when(inner == 0)
-        def _():
-            sent(zos.at[c, :, y], 17 + 2 * t)
-            sent(eos.at[c, :, y], 18 + 2 * t)
-
-        @pl.when(inner == 1)
-        def _():
-            sent(qbuf.at[c, 0, y, pl.ds(0, 2)], 2 + t)
-            sent(zfs.at[c, :, y], 21 + 2 * t)
-            sent(efs.at[c, :, y], 22 + 2 * t)
-
-    sent(qbuf.at[:, 0], 6)
-    sent(p1s, 7)
-    sent(e1s, 8)
+    def sent_of(n, *pairs):
+        if n:
+            for fn, si in pairs:
+                sent(fn(upto(n)), si)
+
+    na, nbb = (Q_WAY.count(w) for w in "AB")
+    sent_of(na, (lambda c: qbuf.at[c, 0, 0, upto(2)], 1))
+    sent_of(nbb, (lambda c: qbuf.at[c, 0, :, upto(2)], 3), (lambda c: qbuf.at[c, 0, 0, 0], 6))
+    sent_of(na, (lambda c: qbuf.at[c, 0, 0], 5))
+
+    @pl.when(inner == 1)
+    def _():
+        sent_of(na, (lambda c: qbuf.at[c, 0, 0, upto(2)], 2))
+        sent_of(nbb, (lambda c: qbuf.at[c, 0, :, upto(2)], 4))
+
+    sent(qbuf.at[:, 0], 7)
+    od, oa, ob = (O_WAY.count(w) for w in "DAB")
+    sent_of(od + oa, (lambda c: ys.at[c], 10), (lambda c: eys.at[c], 11),
+            (lambda c: zns.at[c, 0], 14), (lambda c: ens.at[c, 0], 15))
+    sent_of(ob, (lambda c: ys.at[c, 0], 12), (lambda c: eys.at[c, 0], 13),
+            (lambda c: zns.at[c], 16), (lambda c: ens.at[c], 17))
+
+    @pl.when(inner == 0)
+    def _():
+        sent_of(od + oa, (lambda c: zos.at[c, :, 0], 18), (lambda c: eos.at[c, :, 0], 19))
+        sent_of(ob, (lambda c: zos.at[c], 20), (lambda c: eos.at[c], 21))
+
+    @pl.when(inner == 1)
+    def _():
+        sent_of(od, (lambda c: zos.at[c, :, 0], 18), (lambda c: eos.at[c, :, 0], 19))
+        sent_of(oa, (lambda c: zfs.at[c, :, 0], 22), (lambda c: efs.at[c, :, 0], 23))
+        sent_of(ob, (lambda c: zfs.at[c], 24), (lambda c: efs.at[c], 25))
+
+    sent(p1s, 8)
+    sent(e1s, 9)
+    pltpu.make_async_copy(out_ref, out_ref, osem).wait()
 
 
 def solution(mesh):
@@ -433,7 +472,7 @@
             functools.partial(fused, nb, own, span, dim),
             out_shape=jax.ShapeDtypeStruct((own, nb, dim), BF16),
             in_specs=[pl.BlockSpec(memory_space=pltpu.SMEM), any_spec, any_spec, any_spec],
-            out_specs=pl.BlockSpec(memory_space=vm),
+            out_specs=any_spec,
             scratch_shapes=[
                 vm((nb, span, dim), BF16), vm((nb, span, dim), BF16),
                 blocks(2, 2, 4),
@@ -446,7 +485,7 @@
                 blocks(4), blocks(4), blocks(2), blocks(2),
                 blocks(2, 2), blocks(2, 2), blocks(2, 2), blocks(2),
                 line(4), line(4), line(2), line(2), line(2, 2), line(2, 2), line(2, 2), line(2),
-                dma((nc,)), dma, dma((25,)), dma((4, nc)), dma((10, nc)),
+                blocks(), dma((nc,)), dma, dma, dma((26,)), dma((4, nc)), dma((10, nc)),
             ],
             compiler_params=pltpu.CompilerParams(
                 collective_id=0, has_side_effects=True, vmem_limit_bytes=67043328),

time: 56.3 us -> 52.2 us (0.927)
  Pallas kernels: 54.5 us -> 50.4 us
    pallas_call x1, Pallas kernels: 54.5 us -> 50.4 us  [group_step(): pl.pallas_call(functools.partial(fused, nb, own, span, dim), out_shape=ja...]
where the time goes in v4:
time: 52.2 us; the launch traced here: 52.1 us
  Pallas kernels  50.4 us (97%)
  local copies, waits for them, and re-layouts  1.62 us (3%)
    pallas_call x1, Pallas kernels, group_step(): pl.pallas_call(functools.partial(fused, nb, own, span, dim), out_shape=ja...  50.4 us
    unnamed x1, local copies, waits for them, and re-layouts  1.62 us

profile of v4, /device:TPU:0, one launch (start us, length us, event | category | flops | bytes accessed | tf_op | source)
XLA Modules:
  0.0 52.1 jit_solution(15302093486218995564)
XLA Ops:
  0.0 50.4 %attend.1 = bf16[3,256,128]{2,1,0:T(8,128)(2,1)} custom-call(s32[256]{0:T(256)} %len_ref.1, bf16[3,256,128]{2,1,0:T(8,128)(2,1)} %bitcast.3, bf16[256,256,128]{2,1,0:T(8,128)(2,1)} %k_ref.1, bf16[256,256,128]{2,1,0:T(8,128)(2,1)} %v_ref.1), custom_call_target="tpu_custom_call" | custom-call | tf_op jit(solution)/shard_map/attend/pallas_call | solution.py:471
  50.5 1.6 %copy.6 = bf16[256,3,128]{2,0,1:T(8,128)(2,1)} copy(bf16[256,3,128]{2,0,1:T(8,128)(2,1)} %bitcast.2) | data formatting | bytes 393216

commit v5 on v4

--- a/solution.py
+++ b/solution.py
@@ -12,9 +12,9 @@
 UNROLL = 32
 AHEAD = 2
 Y_AHEAD = 3
-LAG = (0, 1, 3, 4, 5, 7, 9, 11)
+LAG = (0, 1, 3, 4, 5, 7, 11)
 Q_WAY = "AAABAABA"
-O_WAY = "DDBDDDDD"
+O_WAY = "DDDDDDDD"
 NEG = -3.4e38
 FLOOR = -3.0e38
 MESH = pl.DeviceIdType.MESH
@@ -23,8 +23,8 @@
 def fused(nb, own, span, dim, len_ref, q_ref, k_ref, v_ref, out_ref,
           kbuf, vbuf, qbuf, qf, of, posm, macc, dacc, sbuf, pbuf,
           p1s, p1r, e1k, e1s, e1r, part, lse, ltmp,
-          ys, yr, zns, znr, zos, zor, zfs, zfr,
-          eys, eyr, ens, enr, eos, eor, efs, efr,
+          ys, yr, zns, znr, zos, zor,
+          eys, eyr, ens, enr, eos, eor,
           obuf, kvsem, qsem, osem, ss, rq, rr):
     nc = CHUNKS
     bc = nb // nc
@@ -278,109 +278,49 @@
 
     def z_send(c, ny):
         y = upto(ny)
-
-        @pl.when(inner == 0)
-        def _():
-            for m in range(2):
-                for h in range(ny):
-                    eos[c, m, h] = lse[c, 4 * h + 2 + m:4 * h + 3 + m]
-                    for i in range(own):
-                        zos[c, m, h, i] = part[c, 4 * h + 2 + m, i].astype(BF16)
-            send(eos.at[c, :, y], eor.at[c, :, y], 17 + ny + ny, rr.at[7, c], z1)
-            send(zos.at[c, :, y], zor.at[c, :, y], 16 + ny + ny, rr.at[6, c], z1)
-
-        for h in range(ny):
-            ens[c, h] = lse[c, 4 * h + 1:4 * h + 2]
-            for i in range(own):
-                zns[c, h, i] = part[c, 4 * h + 1, i].astype(BF16)
+        for k, dat, lin in ((3, zos.at[c, 1], eos.at[c, 1]), (2, zos.at[c, 0], eos.at[c, 0]), (1, zns.at[c], ens.at[c])):
+            for h in range(ny):
+                lin[h] = lse[c, 4 * h + k:4 * h + k + 1]
+                for i in range(own):
+                    dat[h, i] = part[c, 4 * h + k, i].astype(BF16)
+        for m, dev in ((1, z3), (0, z2)):
+            send(eos.at[c, m, y], eor.at[c, m, y], 17 + ny + ny, rr.at[7, c], dev)
+            send(zos.at[c, m, y], zor.at[c, m, y], 16 + ny + ny, rr.at[6, c], dev)
         send(ens.at[c, y], enr.at[c, y], 13 + ny + ny, rr.at[5, c], z1)
         send(zns.at[c, y], znr.at[c, y], 12 + ny + ny, rr.at[4, c], z1)
-
-    def z_send_direct(c):
-        for k, dat, lin in ((2, zos.at[c, 0, 0], eos.at[c, 0, 0]), (3, zos.at[c, 1, 0], eos.at[c, 1, 0]),
-                            (1, zns.at[c, 0], ens.at[c, 0])):
-            lin[...] = lse[c, k:k + 1]
-            for i in range(own):
-                dat[i] = part[c, k, i].astype(BF16)
-        for m, dev in ((1, z3), (0, z2)):
-            send(eos.at[c, m, 0], eor.at[c, m, 0], 19, rr.at[7, c], dev)
-            send(zos.at[c, m, 0], zor.at[c, m, 0], 18, rr.at[6, c], dev)
-        send(ens.at[c, 0], enr.at[c, 0], 15, rr.at[5, c], z1)
-        send(zns.at[c, 0], znr.at[c, 0], 14, rr.at[4, c], z1)
-
-    def z_merge_direct(c):
-        recv(enr.at[c, 0], rr.at[5, c])
-        recv(eor.at[c, :, 0], rr.at[7, c])
-        ls = [lines([(0, ref)]) for ref in (enr[c, 0], eor[c, 0, 0], eor[c, 1, 0])]
-        ws, _ = weights(lse[c], *ls)
-        recv(znr.at[c, 0], rr.at[4, c])
-        recv(zor.at[c, :, 0], rr.at[6, c])
-        for i in range(own):
-            o = cut(ws[0], 0, i) * part[c, 0, i]
-            for w, dat in zip(ws[1:], (znr.at[c, 0], zor.at[c, 0, 0], zor.at[c, 1, 0])):
-                o = o + cut(w, 0, i) * dat[i].astype(F32)
-            finish(c, i, o)
-        ship(c)
-
-    def z_relay(c, ny):
-        y = upto(ny)
-        recv(eor.at[c, :, y], rr.at[7, c])
-        (wa, wb), new = weights(lse[c], lines([(4 * h + 3 - m, eor[c, m, h]) for m in range(2) for h in range(ny)]))
-        recv(zor.at[c, :, y], rr.at[6, c])
-        for m in range(2):
-            for h in range(ny):
-                n = 4 * h + 3 - m
-                efs[c, m, h] = new[n:n + 1]
-                for i in range(own):
-                    o = cut(wa, n, i) * part[c, n, i] + cut(wb, n, i) * zor[c, m, h, i].astype(F32)
-                    zfs[c, m, h, i] = o.astype(BF16)
-        for m, dev in ((1, z2), (0, z3)):
-            send(efs.at[c, m, y], efr.at[c, y], 21 + ny + ny, rr.at[9, c], dev)
-            send(zfs.at[c, m, y], zfr.at[c, y], 20 + ny + ny, rr.at[8, c], dev)
 
     def z_merge(c, ny):
         y = upto(ny)
         recv(enr.at[c, y], rr.at[5, c])
-        recv(efr.at[c, y], rr.at[9, c])
-        near = lines([(4 * h, enr[c, h]) for h in range(ny)])
-        far = lines([(4 * h, efr[c, h]) for h in range(ny)])
-        (wa, wb, wc), new = weights(lse[c], near, far)
-        lse[c] = new
+        recv(eor.at[c, :, y], rr.at[7, c])
+        came = ((znr.at[c], enr.at[c]), (zor.at[c, 0], eor.at[c, 0]), (zor.at[c, 1], eor.at[c, 1]))
+        ws, new = weights(lse[c], *[lines([(4 * h, lin[h]) for h in range(ny)]) for _, lin in came])
         recv(znr.at[c, y], rr.at[4, c])
-        recv(zfr.at[c, y], rr.at[8, c])
+        recv(zor.at[c, :, y], rr.at[6, c])
         for h in range(ny):
-            n = 4 * h
             for i in range(own):
-                o = (cut(wa, n, i) * part[c, n, i] + cut(wb, n, i) * znr[c, h, i].astype(F32)
-                     + cut(wc, n, i) * zfr[c, h, i].astype(F32))
+                o = cut(ws[0], 4 * h, i) * part[c, 4 * h, i]
+                for w, (dat, _) in zip(ws[1:], came):
+                    o = o + cut(w, 4 * h, i) * dat[h, i].astype(F32)
                 if ny == 1:
                     finish(c, i, o)
                 else:
-                    part[c, n, i] = o
+                    part[c, 4 * h, i] = o
         if ny == 1:
             ship(c)
-
-    r0_send = by_way(O_WAY, {"D": lambda c: y_send(c, 1), "A": lambda c: y_send(c, 1), "B": lambda c: z_send(c, 2)})
+        else:
+            lse[c] = new
+
+    r0_send = by_way(O_WAY, {"D": lambda c: y_send(c, 1), "E": lambda c: z_send(c, 2)})
 
     def r0(c):
         merge_partner(c)
         r0_send(c)
 
-    def relay(c, ny):
-        pl.when(inner == 1)(lambda: z_relay(c, ny))
-
     r1 = by_way(O_WAY, {
-        "D": both(lambda c: y_merge(c, 1), z_send_direct),
-        "A": both(lambda c: y_merge(c, 1), lambda c: z_send(c, 1)),
-        "B": lambda c: relay(c, 2)})
-    r2 = by_way(O_WAY, {
-        "D": None,
-        "A": lambda c: relay(c, 1),
-        "B": both(lambda c: z_merge(c, 2), lambda c: y_send(c, 2))})
-    r3 = by_way(O_WAY, {
-        "D": z_merge_direct,
-        "A": lambda c: z_merge(c, 1),
-        "B": lambda c: y_merge(c, 2)})
+        "D": both(lambda c: y_merge(c, 1), lambda c: z_send(c, 1)),
+        "E": both(lambda c: z_merge(c, 2), lambda c: y_send(c, 2))})
+    r2 = by_way(O_WAY, {"D": lambda c: z_merge(c, 1), "E": lambda c: y_merge(c, 2)})
 
     def at(c, fn):
         pl.when((c >= 0) & (c < nc))(lambda: fn(c))
@@ -402,10 +342,9 @@
         at(st - LAG[4], r0)
         at(st - LAG[5], r1)
         at(st - LAG[6], r2)
-        at(st - LAG[7], r3)
         return carry
 
-    lax.fori_loop(0, nc + LAG[7], step, 0)
+    lax.fori_loop(0, nc + LAG[6], step, 0)
 
     def sent(ref, si):
         remote(ref, ref, ss.at[si], rq.at[0, 0], partner).wait_send()
@@ -426,22 +365,13 @@
         sent_of(nbb, (lambda c: qbuf.at[c, 0, :, upto(2)], 4))
 
     sent(qbuf.at[:, 0], 7)
-    od, oa, ob = (O_WAY.count(w) for w in "DAB")
-    sent_of(od + oa, (lambda c: ys.at[c], 10), (lambda c: eys.at[c], 11),
-            (lambda c: zns.at[c, 0], 14), (lambda c: ens.at[c, 0], 15))
-    sent_of(ob, (lambda c: ys.at[c, 0], 12), (lambda c: eys.at[c, 0], 13),
-            (lambda c: zns.at[c], 16), (lambda c: ens.at[c], 17))
-
-    @pl.when(inner == 0)
-    def _():
-        sent_of(od + oa, (lambda c: zos.at[c, :, 0], 18), (lambda c: eos.at[c, :, 0], 19))
-        sent_of(ob, (lambda c: zos.at[c], 20), (lambda c: eos.at[c], 21))
-
-    @pl.when(inner == 1)
-    def _():
-        sent_of(od, (lambda c: zos.at[c, :, 0], 18), (lambda c: eos.at[c, :, 0], 19))
-        sent_of(oa, (lambda c: zfs.at[c, :, 0], 22), (lambda c: efs.at[c, :, 0], 23))
-        sent_of(ob, (lambda c: zfs.at[c], 24), (lambda c: efs.at[c], 25))
+    od, oe = (O_WAY.count(w) for w in "DE")
+    sent_of(od, (lambda c: ys.at[c], 10), (lambda c: eys.at[c], 11),
+            (lambda c: zns.at[c, 0], 14), (lambda c: ens.at[c, 0], 15),
+            (lambda c: zos.at[c, :, 0], 18), (lambda c: eos.at[c, :, 0], 19))
+    sent_of(oe, (lambda c: ys.at[c, 0], 12), (lambda c: eys.at[c, 0], 13),
+            (lambda c: zns.at[c], 16), (lambda c: ens.at[c], 17),
+            (lambda c: zos.at[c], 20), (lambda c: eos.at[c], 21))
 
     sent(p1s, 8)
     sent(e1s, 9)
@@ -483,9 +413,9 @@
                 vm((nc, 2, 8, 128), F32), vm((nc, 2, 8, 128), F32), vm((nc, 2, 8, 128), F32),
                 vm((nc, 8, own, bc, dim), F32), vm((nc, 8, 128), F32), vm((8, 128), F32),
                 blocks(4), blocks(4), blocks(2), blocks(2),
-                blocks(2, 2), blocks(2, 2), blocks(2, 2), blocks(2),
-                line(4), line(4), line(2), line(2), line(2, 2), line(2, 2), line(2, 2), line(2),
-                blocks(), dma((nc,)), dma, dma, dma((26,)), dma((4, nc)), dma((10, nc)),
+                blocks(2, 2), blocks(2, 2),
+                line(4), line(4), line(2), line(2), line(2, 2), line(2, 2),
+                blocks(), dma((nc,)), dma, dma, dma((22,)), dma((4, nc)), dma((8, nc)),
             ],
             compiler_params=pltpu.CompilerParams(
                 collective_id=0, has_side_effects=True, vmem_limit_bytes=67043328),

time: 52.2 us -> 52.2 us (level)
  no operation moved by 1% of the time
where the time goes in v5:
time: 52.2 us; the launch traced here: 52 us
  Pallas kernels  50.4 us (97%)
  local copies, waits for them, and re-layouts  1.62 us (3%)
    pallas_call x1, Pallas kernels, group_step(): pl.pallas_call(functools.partial(fused, nb, own, span, dim), out_shape=ja...  50.4 us
    unnamed x1, local copies, waits for them, and re-layouts  1.62 us

profile of v5, /device:TPU:0, one launch (start us, length us, event | category | flops | bytes accessed | tf_op | source)
XLA Modules:
  0.0 52.0 jit_solution(3367423995680780570)
XLA Ops:
  0.0 50.4 %attend.1 = bf16[3,256,128]{2,1,0:T(8,128)(2,1)} custom-call(s32[256]{0:T(256)} %len_ref.1, bf16[3,256,128]{2,1,0:T(8,128)(2,1)} %bitcast.3, bf16[256,256,128]{2,1,0:T(8,128)(2,1)} %k_ref.1, bf16[256,256,128]{2,1,0:T(8,128)(2,1)} %v_ref.1), custom_call_target="tpu_custom_call" | custom-call | tf_op jit(solution)/shard_map/attend/pallas_call | solution.py:401
  50.4 1.6 %copy.6 = bf16[256,3,128]{2,0,1:T(8,128)(2,1)} copy(bf16[256,3,128]{2,0,1:T(8,128)(2,1)} %bitcast.2) | data formatting | bytes 393216

commit v6 on v5

--- a/solution.py
+++ b/solution.py
@@ -135,6 +135,12 @@
         z = pl.ds(1, 3)
         send(qbuf.at[c, 0, 0, z], qbuf.at[c, 0, 1, z], 5, rq.at[2, c], ypeer)
 
+    def q_y_if(c, role):
+        @pl.when(inner == role)
+        def _():
+            q_end(c, 1)
+            q_y_rest(c)
+
     def q_partner(c):
         send(qbuf.at[c, 0], qbuf.at[c, 1], 7, rq.at[3, c], partner)
 
@@ -151,10 +157,10 @@
     y_own = by_way(Q_WAY, {"A": q_y_own, "B": lambda c: q_y_own(c, 6)})
     q0 = by_way(Q_WAY, {"A": lambda c: q_far(c, 1)})
     q1 = by_way(Q_WAY, {
-        "A": lambda c: q_relay(c, 1),
+        "A": both(lambda c: q_relay(c, 1), lambda c: q_y_if(c, 1)),
         "B": both(lambda c: recv(qbuf.at[c, 0, 1, 0], rq.at[2, c]), lambda c: q_far(c, 2))})
     q2 = by_way(Q_WAY, {
-        "A": both(lambda c: q_end(c, 1), q_y_rest),
+        "A": lambda c: q_y_if(c, 0),
         "B": lambda c: q_relay(c, 2)})
     q3 = by_way(Q_WAY, {
         "A": q_last,

time: 52.2 us -> 52.2 us (level)
  no operation moved by 1% of the time
where the time goes in v6:
time: 52.2 us; the launch traced here: 52 us
  Pallas kernels  50.4 us (97%)
  local copies, waits for them, and re-layouts  1.62 us (3%)
    pallas_call x1, Pallas kernels, group_step(): pl.pallas_call(functools.partial(fused, nb, own, span, dim), out_shape=ja...  50.4 us
    unnamed x1, local copies, waits for them, and re-layouts  1.62 us

profile of v6, /device:TPU:0, one launch (start us, length us, event | category | flops | bytes accessed | tf_op | source)
XLA Modules:
  0.0 52.0 jit_solution(6018489395219929697)
XLA Ops:
  0.0 50.4 %attend.1 = bf16[3,256,128]{2,1,0:T(8,128)(2,1)} custom-call(s32[256]{0:T(256)} %len_ref.1, bf16[3,256,128]{2,1,0:T(8,128)(2,1)} %bitcast.3, bf16[256,256,128]{2,1,0:T(8,128)(2,1)} %k_ref.1, bf16[256,256,128]{2,1,0:T(8,128)(2,1)} %v_ref.1), custom_call_target="tpu_custom_call" | custom-call | tf_op jit(solution)/shard_map/attend/pallas_call | solution.py:407
  50.4 1.6 %copy.6 = bf16[256,3,128]{2,0,1:T(8,128)(2,1)} copy(bf16[256,3,128]{2,0,1:T(8,128)(2,1)} %bitcast.2) | data formatting | bytes 393216
